TPU v7x, 256 devices: a whole 4x4x8 slice. The times are simulated.
256 devices in a mesh: rows: 16 (over y, x), tp: 16 (over z, core).
Axes of the slice: x: 4, y: 4, z: 8, core: 2. Of those that a mesh axis runs over, the one named last changes fastest.
Arguments:
- train_gate: float32 [3584, 14336], P('rows', 'tp'), may hold values from -0.125 to 0.125
- drift_gate: float32 [3584, 14336], P('rows', 'tp'), may hold values from -6 to 6
- spread_gate: float32 [3584, 14336], P('rows', 'tp'), may hold values from 0.1 to 10
- train_up: float32 [3584, 14336], P('rows', 'tp'), may hold values from -0.125 to 0.125
- drift_up: float32 [3584, 14336], P('rows', 'tp'), may hold values from -6 to 6
- spread_up: float32 [3584, 14336], P('rows', 'tp'), may hold values from 0.1 to 10
- norm_gain: float32 [3584], P('rows'), may hold values from 0.25 to 1.75
Outputs:
- serving_gate: bfloat16 [3584, 14336], P(None, 'tp')
- serving_up: bfloat16 [3584, 14336], P(None, 'tp')
- column_gate: float32 [14336], P('tp')
- column_up: float32 [14336], P('tp')
All inputs are finite; a program needn't handle non-finite values. Where the computation divides by a largest or mean magnitude, that divisor is 1e-20 or more.
Results may differ from a plain program's by a relative error of at most 0.001.
Values may be sent and summed in bfloat16 or wider, within the bound.
No kernel may reach another device: no remote copies, remote signals or barrier semaphores. Data moves between devices by JAX's collectives and lax.ppermute only.
A program may use at most 128 MiB of HBM per device.

v0:
```python
import jax
import jax.numpy as jnp
from jax import lax
from jax.experimental import pallas as pl
from jax.experimental.pallas import tpu as pltpu
from jax.sharding import PartitionSpec as P

learn_rate = 0.015
decay_rate = 0.1
tiny_value = 1e-08
SIDE = 4
TP = 16


def send(value, dy, dx):
    pairs = []
    for y in range(SIDE):
        for x in range(SIDE):
            for t in range(TP):
                s = 1 - 2 * (t % 2)
                to = ((y + s * dy) % SIDE) * SIDE + (x + s * dx) % SIDE
                pairs.append(((y * SIDE + x) * TP + t, to * TP + t))
    return lax.ppermute(value, ("rows", "tp"), pairs)


def place(outs, pieces):
    blocks = [pltpu.with_memory_space_constraint(p[3], pltpu.VMEM) for p in pieces]
    rows = outs[0].shape[0] // (SIDE * SIDE)

    def body(*refs):
        n = len(blocks)
        ins = refs[2 : 2 + n]
        dst = refs[2 + n : 4 + n]
        sems = refs[-1]
        r = lax.axis_index("rows")
        s = 1 - 2 * (lax.axis_index("tp") % 2)
        y, x = r // SIDE, r % SIDE
        copies = []
        for k, (which, dy, dx, block, first) in enumerate(pieces):
            at = ((y + s * dy + 2 * SIDE) % SIDE) * SIDE + (x + s * dx + 2 * SIDE) % SIDE
            there = pl.ds(at * rows + first, block.shape[0])
            copies.append(pltpu.make_async_copy(ins[k], dst[which].at[there, :], sems.at[k]))
        for c in copies:
            c.start()
        for c in copies:
            c.wait()

    any_spec = pl.BlockSpec(memory_space=pl.ANY)
    return pl.pallas_call(
        body,
        out_shape=tuple(jax.ShapeDtypeStruct(o.shape, o.dtype) for o in outs),
        in_specs=[any_spec] * (2 + len(blocks)),
        out_specs=(any_spec, any_spec),
        input_output_aliases={0: 0, 1: 1},
        scratch_shapes=[pltpu.SemaphoreType.DMA((len(blocks),))],
        compiler_params=pltpu.CompilerParams(vmem_limit_bytes=1 << 20),
    )(*outs, *blocks)


def blank(shape, dtype):
    return pl.pallas_call(
        lambda a, b: None,
        out_shape=(jax.ShapeDtypeStruct(shape, dtype),) * 2,
        out_specs=(pl.BlockSpec(memory_space=pl.ANY),) * 2,
        compiler_params=pltpu.CompilerParams(vmem_limit_bytes=1 << 20),
    )()


def stepped(train, drift, spread):
    return train - learn_rate * (drift / (jnp.sqrt(spread) + tiny_value) + decay_rate * train)


def coded(value, peak):
    part = value * (1.0 / peak)
    return lax.optimization_barrier((part * jnp.abs(part) * TOP).astype(jnp.float16))


def decoded(code, scale):
    code = code.astype(jnp.float32)
    return (code * lax.rsqrt(jnp.maximum(jnp.abs(code), SMALL)) * scale).astype(jnp.bfloat16)


SMALL = 1e-30
TOP = 32768.0

SLOTS = (
    (("gx1", "g", 0, 1), ("uy1", "u", 1, 0), ("ux1", "u", 0, 1), ("gy1", "g", 1, 0)),
    (("gx2", "g", 0, -1), ("uy2", "u", -1, 0), ("ux2", "u", 0, -1), ("gy2", "g", -1, 0)),
    (("gx3", "gx1", 0, 1), ("uy3", "uy1", 1, 0), ("u11", "uy1", 0, 1), ("g11", "gx1", 1, 0)),
    (("u22", "uy2", 0, -1), ("g22", "gx2", -1, 0), ("ux3", "ux2", 0, -1), ("gy3", "gy2", -1, 0)),
    (("u31", "uy3", 0, 1), ("g31", "gx3", 1, 0), ("u21", "uy2", 0, 1), ("g21", "gx2", 1, 0)),
    (("u32", "uy3", 0, -1), ("g32", "gx3", -1, 0), ("u23", "u22", 0, -1), ("g23", "g22", -1, 0)),
    (("u33", "u31", 0, 1), ("g33", "g31", 1, 0), ("u13", "u11", 0, 1), ("g13", "g11", 1, 0)),
    (("u12", "uy1", 0, -1), ("g12", "gx1", -1, 0)),
)
ROUTE = tuple(r for slot in SLOTS for r in slot)
ORIGIN = {"g": (0, 0), "u": (0, 0)}
BATCHES = [tuple(ORIGIN) + tuple(r[0] for r in SLOTS[0])] + [tuple(r[0] for r in slot) for slot in SLOTS[1:]]
for _name, _source, _dy, _dx in ROUTE:
    _y, _x = ORIGIN[_source]
    ORIGIN[_name] = (_y - _dy, _x - _dx)


def per_device(train_gate, drift_gate, spread_gate, train_up, drift_up, spread_up, norm_gain):
    rows, width = train_gate.shape
    gate = stepped(train_gate, drift_gate, spread_gate) * norm_gain[:, None]
    up = stepped(train_up, drift_up, spread_up) * norm_gain[:, None]
    peak_gate, peak_up = (jnp.maximum(jnp.max(jnp.abs(v), axis=0), SMALL) for v in (gate, up))
    have = {"g": coded(gate, peak_gate), "u": coded(up, peak_up)}
    peak = jnp.concatenate([peak_gate, peak_up])
    peaks = jnp.broadcast_to(peak, (SIDE * SIDE, 2 * width))
    peaks = lax.all_to_all(peaks, "rows", 0, 0, tiled=True)
    column = jnp.max(peaks, axis=0)
    column_gate, column_up = column[:width], column[width:]
    scales = peaks * (TOP**-0.5 / column)
    outs = blank((rows * SIDE * SIDE, width), jnp.bfloat16)
    for name, source, dy, dx in ROUTE:
        have[name] = send(have[source], dy, dx)
    at = lax.axis_index("rows")
    sense = 1 - 2 * (lax.axis_index("tp") % 2)

    def scale_of(name):
        dy, dx = ORIGIN[name]
        y = (at // SIDE + sense * dy + 2 * SIDE) % SIDE
        x = (at % SIDE + sense * dx + 2 * SIDE) % SIDE
        low = width * (name[0] == "u")
        return lax.dynamic_slice(scales, (y * SIDE + x, low), (1, width))

    for batch in BATCHES:
        pieces = [(int(n[0] == "u"), *ORIGIN[n], decoded(have[n], scale_of(n)), 0) for n in batch]
        outs = place(outs, pieces)
    return (*outs, column_gate, column_up)


def solution(mesh):
    return jax.shard_map(
        per_device,
        mesh=mesh,
        in_specs=(P("rows", "tp"),) * 6 + (P("rows"),),
        out_specs=(P(None, "tp"), P(None, "tp"), P("tp"), P("tp")),
        check_vma=False,
    )
```

profile of v0, /device:TPU:140, one launch (start us, length us, event | category | flops | bytes accessed | tf_op | source)
XLA Modules:
  0.0 105.6 jit_solution(5039157057717404621)
XLA Ops:
  0.6 3.2 %abs_reduce_fusion = (f32[896]{0:T(1024)S(1)}, f32[224,896]{1,0:T(8,128)S(1)}, f32[896]{0:T(1024)S(1)}, f32[224,896]{1,0:T(8,128)S(1)}) fusion(f32[224]{0:T(256)} %param.13, f32[224,896]{1,0:T(8,128)} %param.10, f32[224,896]{1,0:T(8,128)} %param.11, f32[224,896]{1,0:T(8,128)} %param.12, f32[224,896]{1,0:T(8,128)} %param.7, f32[224,896]{1,0:T(8,128)} %param.8, ...), kind=kLoop, calls=%fused_computation.198 | loop fusion | flops 3610880 | bytes 6430592 | tf_op jit(solution)/shard_map/reduce_max | solution.py:108
  4.0 1.3 %collective-permute-start.2 = (f16[224,896]{1,0:T(8,128)(2,1)S(1)}, f16[224,896]{1,0:T(8,128)(2,1)S(1)}, u32[]{:S(2)}, u32[]{:S(2)}) collective-permute-start(f16[224,896]{1,0:T(8,128)(2,1)S(1)} %fusion.131), channel_id=1, source_target_pairs={{0,16},{1,49},{2,18},{3,51},{4,20},{5,53},{6,22},{7,55},{8,24},{9,... | collective-permute-start | bytes 1204232 | tf_op jit(solution)/shard_map/ppermute | solution.py:23
  5.3 1.6 %collective-permute-start.1 = (f16[224,896]{1,0:T(8,128)(2,1)S(1)}, f16[224,896]{1,0:T(8,128)(2,1)S(1)}, u32[]{:S(2)}, u32[]{:S(2)}) collective-permute-start(f16[224,896]{1,0:T(8,128)(2,1)S(1)} %fusion.131), channel_id=1, source_target_pairs={{0,64},{1,193},{2,66},{3,195},{4,68},{5,197},{6,70},{7,199},{8,72}... | collective-permute-start | bytes 1204232 | tf_op jit(solution)/shard_map/ppermute | solution.py:23
  7.6 7.0 %all-to-all-start = ((f32[16,1,1792]{2,1,0:T(1,128)}), f32[16,1,1792]{2,1,0:T(1,128)S(1)}, u32[]{:S(2)}, u32[]{:S(2)}) async-start(f32[16,1,1792]{2,1,0:T(1,128)} %broadcast_in_dim.2), calls=%async_computation | async-start | bytes 229376 | tf_op jit(solution)/shard_map/all_to_all | solution.py:112
  14.8 1.5 %collective-permute-start.3 = (f16[224,896]{1,0:T(8,128)(2,1)S(1)}, f16[224,896]{1,0:T(8,128)(2,1)S(1)}, u32[]{:S(2)}, u32[]{:S(2)}) collective-permute-start(f16[224,896]{1,0:T(8,128)(2,1)S(1)} %fusion.129), channel_id=1, source_target_pairs={{0,64},{1,193},{2,66},{3,195},{4,68},{5,197},{6,70},{7,199},{8,72}... | collective-permute-start | bytes 1204232 | tf_op jit(solution)/shard_map/ppermute | solution.py:23
  18.3 1.5 %all-to-all-done = f32[16,1,1792]{2,1,0:T(1,128)S(1)} async-done(((f32[16,1,1792]{2,1,0:T(1,128)}), f32[16,1,1792]{2,1,0:T(1,128)S(1)}, u32[]{:S(2)}, u32[]{:S(2)}) %all-to-all-start) | async-done | bytes 114720 | tf_op jit(solution)/shard_map/all_to_all | solution.py:112
  21.3 1.4 %collective-permute-done.3 = f16[224,896]{1,0:T(8,128)(2,1)S(1)} collective-permute-done((f16[224,896]{1,0:T(8,128)(2,1)S(1)}, f16[224,896]{1,0:T(8,128)(2,1)S(1)}, u32[]{:S(2)}, u32[]{:S(2)}) %collective-permute-start.3) | collective-permute-done | bytes 401440 | tf_op jit(solution)/shard_map/ppermute | solution.py:23
  22.7 2.0 %collective-permute-start.5 = (f16[224,896]{1,0:T(8,128)(2,1)S(1)}, f16[224,896]{1,0:T(8,128)(2,1)S(1)}, u32[]{:S(2)}, u32[]{:S(2)}) collective-permute-start(f16[224,896]{1,0:T(8,128)(2,1)S(1)} %fusion.131), channel_id=1, source_target_pairs={{0,192},{1,65},{2,194},{3,67},{4,196},{5,69},{6,198},{7,71},{8,200... | collective-permute-start | bytes 1204232 | tf_op jit(solution)/shard_map/ppermute | solution.py:23
  25.9 1.3 %collective-permute-start.7 = (f16[224,896]{1,0:T(8,128)(2,1)S(1)}, f16[224,896]{1,0:T(8,128)(2,1)S(1)}, u32[]{:S(2)}, u32[]{:S(2)}) collective-permute-start(f16[224,896]{1,0:T(8,128)(2,1)S(1)} %fusion.129), channel_id=1, source_target_pairs={{0,192},{1,65},{2,194},{3,67},{4,196},{5,69},{6,198},{7,71},{8,200... | collective-permute-start | bytes 1204232 | tf_op jit(solution)/shard_map/ppermute | solution.py:23
  27.6 1.5 %shard_map.103 = (bf16[3584,896]{1,0:T(8,128)(2,1)}, bf16[3584,896]{1,0:T(8,128)(2,1)}) custom-call(bf16[3584,896]{1,0:T(8,128)(2,1)} %get-tuple-element.22.refs_0_, bf16[3584,896]{1,0:T(8,128)(2,1)} %get-tuple-element.23.refs_1_, bf16[224,896]{1,0:T(8,128)(2,1)S(1)} %fusion.3.refs_2_, ...), custom_call_target="tpu_custom_call", output_to_operand_aliasing={{0}: (0, {}), {1}: (1, {})} | custom-call | tf_op jit(solution)/shard_map/pallas_call | solution.py:49
  29.1 1.5 %collective-permute-start.8 = (f16[224,896]{1,0:T(8,128)(2,1)S(1)}, f16[224,896]{1,0:T(8,128)(2,1)S(1)}, u32[]{:S(2)}, u32[]{:S(2)}) collective-permute-start(f16[224,896]{1,0:T(8,128)(2,1)S(1)} %collective-permute-done), channel_id=1, source_target_pairs={{0,16},{1,49},{2,18},{3,51},{4,20},{5,53},{6,22},{7,55},{8,24},{9,... | collective-permute-start | bytes 1204232 | tf_op jit(solution)/shard_map/ppermute | solution.py:23
  32.1 3.4 %collective-permute-done.6 = f16[224,896]{1,0:T(8,128)(2,1)S(1)} collective-permute-done((f16[224,896]{1,0:T(8,128)(2,1)S(1)}, f16[224,896]{1,0:T(8,128)(2,1)S(1)}, u32[]{:S(2)}, u32[]{:S(2)}) %collective-permute-start.6) | collective-permute-done | bytes 401440 | tf_op jit(solution)/shard_map/ppermute | solution.py:23
  35.7 4.8 %collective-permute-done.7 = f16[224,896]{1,0:T(8,128)(2,1)S(1)} collective-permute-done((f16[224,896]{1,0:T(8,128)(2,1)S(1)}, f16[224,896]{1,0:T(8,128)(2,1)S(1)}, u32[]{:S(2)}, u32[]{:S(2)}) %collective-permute-start.7) | collective-permute-done | bytes 401440 | tf_op jit(solution)/shard_map/ppermute | solution.py:23
  42.3 1.9 %collective-permute-start.11 = (f16[224,896]{1,0:T(8,128)(2,1)S(1)}, f16[224,896]{1,0:T(8,128)(2,1)S(1)}, u32[]{:S(2)}, u32[]{:S(2)}) collective-permute-start(f16[224,896]{1,0:T(8,128)(2,1)S(1)} %collective-permute-done), channel_id=1, source_target_pairs={{0,64},{1,193},{2,66},{3,195},{4,68},{5,197},{6,70},{7,199},{8,72}... | collective-permute-start | bytes 1204232 | tf_op jit(solution)/shard_map/ppermute | solution.py:23
  47.0 6.2 %collective-permute-done.10 = f16[224,896]{1,0:T(8,128)(2,1)S(1)} collective-permute-done((f16[224,896]{1,0:T(8,128)(2,1)S(1)}, f16[224,896]{1,0:T(8,128)(2,1)S(1)}, u32[]{:S(2)}, u32[]{:S(2)}) %collective-permute-start.10) | collective-permute-done | bytes 401440 | tf_op jit(solution)/shard_map/ppermute | solution.py:23
  53.2 1.6 %collective-permute-start.15 = (f16[224,896]{1,0:T(8,128)(2,1)S(1)}, f16[224,896]{1,0:T(8,128)(2,1)S(1)}, u32[]{:S(2)}, u32[]{:S(2)}) collective-permute-start(f16[224,896]{1,0:T(8,128)(2,1)S(1)} %collective-permute-done.7), channel_id=1, source_target_pairs={{0,192},{1,65},{2,194},{3,67},{4,196},{5,69},{6,198},{7,71},{8,200... | collective-permute-start | bytes 1204232 | tf_op jit(solution)/shard_map/ppermute | solution.py:23
  55.0 1.3 %collective-permute-start.18 = (f16[224,896]{1,0:T(8,128)(2,1)S(1)}, f16[224,896]{1,0:T(8,128)(2,1)S(1)}, u32[]{:S(2)}, u32[]{:S(2)}) collective-permute-start(f16[224,896]{1,0:T(8,128)(2,1)S(1)} %collective-permute-done.5), channel_id=1, source_target_pairs={{0,16},{1,49},{2,18},{3,51},{4,20},{5,53},{6,22},{7,55},{8,24},{9,... | collective-permute-start | bytes 1204232 | tf_op jit(solution)/shard_map/ppermute | solution.py:23
  56.5 1.2 %shard_map.105 = (bf16[3584,896]{1,0:T(8,128)(2,1)}, bf16[3584,896]{1,0:T(8,128)(2,1)}) custom-call(bf16[3584,896]{1,0:T(8,128)(2,1)} %get-tuple-element.26.refs_0_, bf16[3584,896]{1,0:T(8,128)(2,1)} %get-tuple-element.27.refs_1_, bf16[224,896]{1,0:T(8,128)(2,1)S(1)} %fusion.43.refs_2_, ...), custom_call_target="tpu_custom_call", output_to_operand_aliasing={{0}: (0, {}), {1}: (1, {})} | custom-call | tf_op jit(solution)/shard_map/pallas_call | solution.py:49
  59.5 2.0 %collective-permute-start.29 = (f16[224,896]{1,0:T(8,128)(2,1)S(1)}, f16[224,896]{1,0:T(8,128)(2,1)S(1)}, u32[]{:S(2)}, u32[]{:S(2)}) collective-permute-start(f16[224,896]{1,0:T(8,128)(2,1)S(1)} %collective-permute-done), channel_id=1, source_target_pairs={{0,192},{1,65},{2,194},{3,67},{4,196},{5,69},{6,198},{7,71},{8,200... | collective-permute-start | bytes 1204232 | tf_op jit(solution)/shard_map/ppermute | solution.py:23
  61.7 3.4 %collective-permute-done.15 = f16[224,896]{1,0:T(8,128)(2,1)S(1)} collective-permute-done((f16[224,896]{1,0:T(8,128)(2,1)S(1)}, f16[224,896]{1,0:T(8,128)(2,1)S(1)}, u32[]{:S(2)}, u32[]{:S(2)}) %collective-permute-start.15) | collective-permute-done | bytes 401440 | tf_op jit(solution)/shard_map/ppermute | solution.py:23
  66.7 2.0 %collective-permute-start.17 = (f16[224,896]{1,0:T(8,128)(2,1)S(1)}, f16[224,896]{1,0:T(8,128)(2,1)S(1)}, u32[]{:S(2)}, u32[]{:S(2)}) collective-permute-start(f16[224,896]{1,0:T(8,128)(2,1)S(1)} %collective-permute-done.8), channel_id=1, source_target_pairs={{0,64},{1,193},{2,66},{3,195},{4,68},{5,197},{6,70},{7,199},{8,72}... | collective-permute-start | bytes 1204232 | tf_op jit(solution)/shard_map/ppermute | solution.py:23
  68.9 1.7 %collective-permute-done.19 = f16[224,896]{1,0:T(8,128)(2,1)S(1)} collective-permute-done((f16[224,896]{1,0:T(8,128)(2,1)S(1)}, f16[224,896]{1,0:T(8,128)(2,1)S(1)}, u32[]{:S(2)}, u32[]{:S(2)}) %collective-permute-start.19) | collective-permute-done | bytes 401440 | tf_op jit(solution)/shard_map/ppermute | solution.py:23
  70.5 3.2 %collective-permute-start.23 = (f16[224,896]{1,0:T(8,128)(2,1)S(1)}, f16[224,896]{1,0:T(8,128)(2,1)S(1)}, u32[]{:S(2)}, u32[]{:S(2)}) collective-permute-start(f16[224,896]{1,0:T(8,128)(2,1)S(1)} %collective-permute-done.13), channel_id=1, source_target_pairs={{0,192},{1,65},{2,194},{3,67},{4,196},{5,69},{6,198},{7,71},{8,200... | collective-permute-start | bytes 1204232 | tf_op jit(solution)/shard_map/ppermute | solution.py:23
  75.9 1.9 %collective-permute-start.22 = (f16[224,896]{1,0:T(8,128)(2,1)S(1)}, f16[224,896]{1,0:T(8,128)(2,1)S(1)}, u32[]{:S(2)}, u32[]{:S(2)}) collective-permute-start(f16[224,896]{1,0:T(8,128)(2,1)S(1)} %collective-permute-done.12), channel_id=1, source_target_pairs={{0,48},{1,17},{2,50},{3,19},{4,52},{5,21},{6,54},{7,23},{8,56},{9,... | collective-permute-start | bytes 1204232 | tf_op jit(solution)/shard_map/ppermute | solution.py:23
  77.9 2.3 %collective-permute-start.26 = (f16[224,896]{1,0:T(8,128)(2,1)S(1)}, f16[224,896]{1,0:T(8,128)(2,1)S(1)}, u32[]{:S(2)}, u32[]{:S(2)}) collective-permute-start(f16[224,896]{1,0:T(8,128)(2,1)S(1)} %collective-permute-done.10), channel_id=1, source_target_pairs={{0,16},{1,49},{2,18},{3,51},{4,20},{5,53},{6,22},{7,55},{8,24},{9,... | collective-permute-start | bytes 1204232 | tf_op jit(solution)/shard_map/ppermute | solution.py:23
  82.9 4.2 %collective-permute-done.21 = f16[224,896]{1,0:T(8,128)(2,1)S(1)} collective-permute-done((f16[224,896]{1,0:T(8,128)(2,1)S(1)}, f16[224,896]{1,0:T(8,128)(2,1)S(1)}, u32[]{:S(2)}, u32[]{:S(2)}) %collective-permute-start.21) | collective-permute-done | bytes 401440 | tf_op jit(solution)/shard_map/ppermute | solution.py:23
  87.3 3.1 %collective-permute-done.22 = f16[224,896]{1,0:T(8,128)(2,1)S(1)} collective-permute-done((f16[224,896]{1,0:T(8,128)(2,1)S(1)}, f16[224,896]{1,0:T(8,128)(2,1)S(1)}, u32[]{:S(2)}, u32[]{:S(2)}) %collective-permute-start.22) | collective-permute-done | bytes 401440 | tf_op jit(solution)/shard_map/ppermute | solution.py:23
  90.6 1.2 %shard_map.108 = (bf16[3584,896]{1,0:T(8,128)(2,1)}, bf16[3584,896]{1,0:T(8,128)(2,1)}) custom-call(bf16[3584,896]{1,0:T(8,128)(2,1)} %get-tuple-element.32.refs_0_, bf16[3584,896]{1,0:T(8,128)(2,1)} %get-tuple-element.33.refs_1_, bf16[224,896]{1,0:T(8,128)(2,1)S(1)} %fusion.91.refs_2_, ...), custom_call_target="tpu_custom_call", output_to_operand_aliasing={{0}: (0, {}), {1}: (1, {})} | custom-call | tf_op jit(solution)/shard_map/pallas_call | solution.py:49
  91.8 3.4 %collective-permute-start.24 = (f16[224,896]{1,0:T(8,128)(2,1)S(1)}, f16[224,896]{1,0:T(8,128)(2,1)S(1)}, u32[]{:S(2)}, u32[]{:S(2)}) collective-permute-start(f16[224,896]{1,0:T(8,128)(2,1)S(1)} %collective-permute-done.16), channel_id=1, source_target_pairs={{0,16},{1,49},{2,18},{3,51},{4,20},{5,53},{6,22},{7,55},{8,24},{9,... | collective-permute-start | bytes 1204232 | tf_op jit(solution)/shard_map/ppermute | solution.py:23
  95.6 5.0 %collective-permute-done.24 = f16[224,896]{1,0:T(8,128)(2,1)S(1)} collective-permute-done((f16[224,896]{1,0:T(8,128)(2,1)S(1)}, f16[224,896]{1,0:T(8,128)(2,1)S(1)}, u32[]{:S(2)}, u32[]{:S(2)}) %collective-permute-start.24) | collective-permute-done | bytes 401440 | tf_op jit(solution)/shard_map/ppermute | solution.py:23
  100.7 2.3 %collective-permute-done.25 = f16[224,896]{1,0:T(8,128)(2,1)S(1)} collective-permute-done((f16[224,896]{1,0:T(8,128)(2,1)S(1)}, f16[224,896]{1,0:T(8,128)(2,1)S(1)}, u32[]{:S(2)}, u32[]{:S(2)}) %collective-permute-start.25) | collective-permute-done | bytes 401440 | tf_op jit(solution)/shard_map/ppermute | solution.py:23
  103.2 1.2 %shard_map.109 = (bf16[3584,896]{1,0:T(8,128)(2,1)}, bf16[3584,896]{1,0:T(8,128)(2,1)}) custom-call(bf16[3584,896]{1,0:T(8,128)(2,1)} %get-tuple-element.34.refs_0_, bf16[3584,896]{1,0:T(8,128)(2,1)} %get-tuple-element.35.refs_1_, bf16[224,896]{1,0:T(8,128)(2,1)S(1)} %fusion.107.refs_2_, ...), custom_call_target="tpu_custom_call", output_to_operand_aliasing={{0}: (0, {}), {1}: (1, {})} | custom-call | tf_op jit(solution)/shard_map/pallas_call | solution.py:49
  (84 shorter events, 23.2 us)
Async XLA Ops:
  4.0 20.9 %collective-permute-start.2 = (f16[224,896]{1,0:T(8,128)(2,1)S(1)}, f16[224,896]{1,0:T(8,128)(2,1)S(1)}, u32[]{:S(2)}, u32[]{:S(2)}) collective-permute-start(f16[224,896]{1,0:T(8,128)(2,1)S(1)} %fusion.131), channel_id=1, source_target_pairs={{0,16},{1,49},{2,18},{3,51},{4,20},{5,53},{6,22},{7,55},{8,24},{9,... | collective-permute-start | bytes 1204232 | tf_op jit(solution)/shard_map/ppermute | solution.py:23
  5.3 20.6 %collective-permute-start.1 = (f16[224,896]{1,0:T(8,128)(2,1)S(1)}, f16[224,896]{1,0:T(8,128)(2,1)S(1)}, u32[]{:S(2)}, u32[]{:S(2)}) collective-permute-start(f16[224,896]{1,0:T(8,128)(2,1)S(1)} %fusion.131), channel_id=1, source_target_pairs={{0,64},{1,193},{2,66},{3,195},{4,68},{5,197},{6,70},{7,199},{8,72}... | collective-permute-start | bytes 1204232 | tf_op jit(solution)/shard_map/ppermute | solution.py:23
  7.6 12.2 %all-to-all-start = ((f32[16,1,1792]{2,1,0:T(1,128)}), f32[16,1,1792]{2,1,0:T(1,128)S(1)}, u32[]{:S(2)}, u32[]{:S(2)}) async-start(f32[16,1,1792]{2,1,0:T(1,128)} %broadcast_in_dim.2), calls=%async_computation | async-start | bytes 229376 | tf_op jit(solution)/shard_map/all_to_all | solution.py:112
  14.8 7.9 %collective-permute-start.3 = (f16[224,896]{1,0:T(8,128)(2,1)S(1)}, f16[224,896]{1,0:T(8,128)(2,1)S(1)}, u32[]{:S(2)}, u32[]{:S(2)}) collective-permute-start(f16[224,896]{1,0:T(8,128)(2,1)S(1)} %fusion.129), channel_id=1, source_target_pairs={{0,64},{1,193},{2,66},{3,195},{4,68},{5,197},{6,70},{7,199},{8,72}... | collective-permute-start | bytes 1204232 | tf_op jit(solution)/shard_map/ppermute | solution.py:23
  16.3 11.1 %collective-permute-start = (f16[224,896]{1,0:T(8,128)(2,1)S(1)}, f16[224,896]{1,0:T(8,128)(2,1)S(1)}, u32[]{:S(2)}, u32[]{:S(2)}) collective-permute-start(f16[224,896]{1,0:T(8,128)(2,1)S(1)} %fusion.129), channel_id=1, source_target_pairs={{0,16},{1,49},{2,18},{3,51},{4,20},{5,53},{6,22},{7,55},{8,24},{9,... | collective-permute-start | bytes 1204232 | tf_op jit(solution)/shard_map/ppermute | solution.py:23
  17.5 13.1 %collective-permute-start.4 = (f16[224,896]{1,0:T(8,128)(2,1)S(1)}, f16[224,896]{1,0:T(8,128)(2,1)S(1)}, u32[]{:S(2)}, u32[]{:S(2)}) collective-permute-start(f16[224,896]{1,0:T(8,128)(2,1)S(1)} %fusion.129), channel_id=1, source_target_pairs={{0,48},{1,17},{2,50},{3,19},{4,52},{5,21},{6,54},{7,23},{8,56},{9,... | collective-permute-start | bytes 1204232 | tf_op jit(solution)/shard_map/ppermute | solution.py:23
  22.7 9.2 %collective-permute-start.5 = (f16[224,896]{1,0:T(8,128)(2,1)S(1)}, f16[224,896]{1,0:T(8,128)(2,1)S(1)}, u32[]{:S(2)}, u32[]{:S(2)}) collective-permute-start(f16[224,896]{1,0:T(8,128)(2,1)S(1)} %fusion.131), channel_id=1, source_target_pairs={{0,192},{1,65},{2,194},{3,67},{4,196},{5,69},{6,198},{7,71},{8,200... | collective-permute-start | bytes 1204232 | tf_op jit(solution)/shard_map/ppermute | solution.py:23
  25.0 10.5 %collective-permute-start.6 = (f16[224,896]{1,0:T(8,128)(2,1)S(1)}, f16[224,896]{1,0:T(8,128)(2,1)S(1)}, u32[]{:S(2)}, u32[]{:S(2)}) collective-permute-start(f16[224,896]{1,0:T(8,128)(2,1)S(1)} %fusion.131), channel_id=1, source_target_pairs={{0,48},{1,17},{2,50},{3,19},{4,52},{5,21},{6,54},{7,23},{8,56},{9,... | collective-permute-start | bytes 1204232 | tf_op jit(solution)/shard_map/ppermute | solution.py:23
  25.9 14.6 %collective-permute-start.7 = (f16[224,896]{1,0:T(8,128)(2,1)S(1)}, f16[224,896]{1,0:T(8,128)(2,1)S(1)}, u32[]{:S(2)}, u32[]{:S(2)}) collective-permute-start(f16[224,896]{1,0:T(8,128)(2,1)S(1)} %fusion.129), channel_id=1, source_target_pairs={{0,192},{1,65},{2,194},{3,67},{4,196},{5,69},{6,198},{7,71},{8,200... | collective-permute-start | bytes 1204232 | tf_op jit(solution)/shard_map/ppermute | solution.py:23
  29.1 16.2 %collective-permute-start.8 = (f16[224,896]{1,0:T(8,128)(2,1)S(1)}, f16[224,896]{1,0:T(8,128)(2,1)S(1)}, u32[]{:S(2)}, u32[]{:S(2)}) collective-permute-start(f16[224,896]{1,0:T(8,128)(2,1)S(1)} %collective-permute-done), channel_id=1, source_target_pairs={{0,16},{1,49},{2,18},{3,51},{4,20},{5,53},{6,22},{7,55},{8,24},{9,... | collective-permute-start | bytes 1204232 | tf_op jit(solution)/shard_map/ppermute | solution.py:23
  30.6 16.1 %collective-permute-start.9 = (f16[224,896]{1,0:T(8,128)(2,1)S(1)}, f16[224,896]{1,0:T(8,128)(2,1)S(1)}, u32[]{:S(2)}, u32[]{:S(2)}) collective-permute-start(f16[224,896]{1,0:T(8,128)(2,1)S(1)} %collective-permute-done.1), channel_id=1, source_target_pairs={{0,64},{1,193},{2,66},{3,195},{4,68},{5,197},{6,70},{7,199},{8,72}... | collective-permute-start | bytes 1204232 | tf_op jit(solution)/shard_map/ppermute | solution.py:23
  41.9 11.3 %collective-permute-start.10 = (f16[224,896]{1,0:T(8,128)(2,1)S(1)}, f16[224,896]{1,0:T(8,128)(2,1)S(1)}, u32[]{:S(2)}, u32[]{:S(2)}) collective-permute-start(f16[224,896]{1,0:T(8,128)(2,1)S(1)} %collective-permute-done.1), channel_id=1, source_target_pairs={{0,16},{1,49},{2,18},{3,51},{4,20},{5,53},{6,22},{7,55},{8,24},{9,... | collective-permute-start | bytes 1204232 | tf_op jit(solution)/shard_map/ppermute | solution.py:23
  42.3 12.7 %collective-permute-start.11 = (f16[224,896]{1,0:T(8,128)(2,1)S(1)}, f16[224,896]{1,0:T(8,128)(2,1)S(1)}, u32[]{:S(2)}, u32[]{:S(2)}) collective-permute-start(f16[224,896]{1,0:T(8,128)(2,1)S(1)} %collective-permute-done), channel_id=1, source_target_pairs={{0,64},{1,193},{2,66},{3,195},{4,68},{5,197},{6,70},{7,199},{8,72}... | collective-permute-start | bytes 1204232 | tf_op jit(solution)/shard_map/ppermute | solution.py:23
  44.1 13.6 %collective-permute-start.12 = (f16[224,896]{1,0:T(8,128)(2,1)S(1)}, f16[224,896]{1,0:T(8,128)(2,1)S(1)}, u32[]{:S(2)}, u32[]{:S(2)}) collective-permute-start(f16[224,896]{1,0:T(8,128)(2,1)S(1)} %collective-permute-done.5), channel_id=1, source_target_pairs={{0,48},{1,17},{2,50},{3,19},{4,52},{5,21},{6,54},{7,23},{8,56},{9,... | collective-permute-start | bytes 1204232 | tf_op jit(solution)/shard_map/ppermute | solution.py:23
  45.3 13.1 %collective-permute-start.13 = (f16[224,896]{1,0:T(8,128)(2,1)S(1)}, f16[224,896]{1,0:T(8,128)(2,1)S(1)}, u32[]{:S(2)}, u32[]{:S(2)}) collective-permute-start(f16[224,896]{1,0:T(8,128)(2,1)S(1)} %collective-permute-done.4), channel_id=1, source_target_pairs={{0,192},{1,65},{2,194},{3,67},{4,196},{5,69},{6,198},{7,71},{8,200... | collective-permute-start | bytes 1204232 | tf_op jit(solution)/shard_map/ppermute | solution.py:23
  46.7 12.9 %collective-permute-start.14 = (f16[224,896]{1,0:T(8,128)(2,1)S(1)}, f16[224,896]{1,0:T(8,128)(2,1)S(1)}, u32[]{:S(2)}, u32[]{:S(2)}) collective-permute-start(f16[224,896]{1,0:T(8,128)(2,1)S(1)} %collective-permute-done.6), channel_id=1, source_target_pairs={{0,48},{1,17},{2,50},{3,19},{4,52},{5,21},{6,54},{7,23},{8,56},{9,... | collective-permute-start | bytes 1204232 | tf_op jit(solution)/shard_map/ppermute | solution.py:23
  53.2 12.0 %collective-permute-start.15 = (f16[224,896]{1,0:T(8,128)(2,1)S(1)}, f16[224,896]{1,0:T(8,128)(2,1)S(1)}, u32[]{:S(2)}, u32[]{:S(2)}) collective-permute-start(f16[224,896]{1,0:T(8,128)(2,1)S(1)} %collective-permute-done.7), channel_id=1, source_target_pairs={{0,192},{1,65},{2,194},{3,67},{4,196},{5,69},{6,198},{7,71},{8,200... | collective-permute-start | bytes 1204232 | tf_op jit(solution)/shard_map/ppermute | solution.py:23
  55.0 11.6 %collective-permute-start.18 = (f16[224,896]{1,0:T(8,128)(2,1)S(1)}, f16[224,896]{1,0:T(8,128)(2,1)S(1)}, u32[]{:S(2)}, u32[]{:S(2)}) collective-permute-start(f16[224,896]{1,0:T(8,128)(2,1)S(1)} %collective-permute-done.5), channel_id=1, source_target_pairs={{0,16},{1,49},{2,18},{3,51},{4,20},{5,53},{6,22},{7,55},{8,24},{9,... | collective-permute-start | bytes 1204232 | tf_op jit(solution)/shard_map/ppermute | solution.py:23
  57.8 12.7 %collective-permute-start.19 = (f16[224,896]{1,0:T(8,128)(2,1)S(1)}, f16[224,896]{1,0:T(8,128)(2,1)S(1)}, u32[]{:S(2)}, u32[]{:S(2)}) collective-permute-start(f16[224,896]{1,0:T(8,128)(2,1)S(1)} %collective-permute-done.4), channel_id=1, source_target_pairs={{0,64},{1,193},{2,66},{3,195},{4,68},{5,197},{6,70},{7,199},{8,72}... | collective-permute-start | bytes 1204232 | tf_op jit(solution)/shard_map/ppermute | solution.py:23
  58.4 15.5 %collective-permute-start.28 = (f16[224,896]{1,0:T(8,128)(2,1)S(1)}, f16[224,896]{1,0:T(8,128)(2,1)S(1)}, u32[]{:S(2)}, u32[]{:S(2)}) collective-permute-start(f16[224,896]{1,0:T(8,128)(2,1)S(1)} %collective-permute-done.1), channel_id=1, source_target_pairs={{0,48},{1,17},{2,50},{3,19},{4,52},{5,21},{6,54},{7,23},{8,56},{9,... | collective-permute-start | bytes 1204232 | tf_op jit(solution)/shard_map/ppermute | solution.py:23
  59.5 14.7 %collective-permute-start.29 = (f16[224,896]{1,0:T(8,128)(2,1)S(1)}, f16[224,896]{1,0:T(8,128)(2,1)S(1)}, u32[]{:S(2)}, u32[]{:S(2)}) collective-permute-start(f16[224,896]{1,0:T(8,128)(2,1)S(1)} %collective-permute-done), channel_id=1, source_target_pairs={{0,192},{1,65},{2,194},{3,67},{4,196},{5,69},{6,198},{7,71},{8,200... | collective-permute-start | bytes 1204232 | tf_op jit(solution)/shard_map/ppermute | solution.py:23
  66.6 9.3 %collective-permute-start.16 = (f16[224,896]{1,0:T(8,128)(2,1)S(1)}, f16[224,896]{1,0:T(8,128)(2,1)S(1)}, u32[]{:S(2)}, u32[]{:S(2)}) collective-permute-start(f16[224,896]{1,0:T(8,128)(2,1)S(1)} %collective-permute-done.9), channel_id=1, source_target_pairs={{0,16},{1,49},{2,18},{3,51},{4,20},{5,53},{6,22},{7,55},{8,24},{9,... | collective-permute-start | bytes 1204232 | tf_op jit(solution)/shard_map/ppermute | solution.py:23
  66.7 11.3 %collective-permute-start.17 = (f16[224,896]{1,0:T(8,128)(2,1)S(1)}, f16[224,896]{1,0:T(8,128)(2,1)S(1)}, u32[]{:S(2)}, u32[]{:S(2)}) collective-permute-start(f16[224,896]{1,0:T(8,128)(2,1)S(1)} %collective-permute-done.8), channel_id=1, source_target_pairs={{0,64},{1,193},{2,66},{3,195},{4,68},{5,197},{6,70},{7,199},{8,72}... | collective-permute-start | bytes 1204232 | tf_op jit(solution)/shard_map/ppermute | solution.py:23
  70.5 11.2 %collective-permute-start.23 = (f16[224,896]{1,0:T(8,128)(2,1)S(1)}, f16[224,896]{1,0:T(8,128)(2,1)S(1)}, u32[]{:S(2)}, u32[]{:S(2)}) collective-permute-start(f16[224,896]{1,0:T(8,128)(2,1)S(1)} %collective-permute-done.13), channel_id=1, source_target_pairs={{0,192},{1,65},{2,194},{3,67},{4,196},{5,69},{6,198},{7,71},{8,200... | collective-permute-start | bytes 1204232 | tf_op jit(solution)/shard_map/ppermute | solution.py:23
  73.9 8.7 %collective-permute-start.20 = (f16[224,896]{1,0:T(8,128)(2,1)S(1)}, f16[224,896]{1,0:T(8,128)(2,1)S(1)}, u32[]{:S(2)}, u32[]{:S(2)}) collective-permute-start(f16[224,896]{1,0:T(8,128)(2,1)S(1)} %collective-permute-done.9), channel_id=1, source_target_pairs={{0,48},{1,17},{2,50},{3,19},{4,52},{5,21},{6,54},{7,23},{8,56},{9,... | collective-permute-start | bytes 1204232 | tf_op jit(solution)/shard_map/ppermute | solution.py:23
  74.2 12.9 %collective-permute-start.21 = (f16[224,896]{1,0:T(8,128)(2,1)S(1)}, f16[224,896]{1,0:T(8,128)(2,1)S(1)}, u32[]{:S(2)}, u32[]{:S(2)}) collective-permute-start(f16[224,896]{1,0:T(8,128)(2,1)S(1)} %collective-permute-done.8), channel_id=1, source_target_pairs={{0,192},{1,65},{2,194},{3,67},{4,196},{5,69},{6,198},{7,71},{8,200... | collective-permute-start | bytes 1204232 | tf_op jit(solution)/shard_map/ppermute | solution.py:23
  75.9 14.5 %collective-permute-start.22 = (f16[224,896]{1,0:T(8,128)(2,1)S(1)}, f16[224,896]{1,0:T(8,128)(2,1)S(1)}, u32[]{:S(2)}, u32[]{:S(2)}) collective-permute-start(f16[224,896]{1,0:T(8,128)(2,1)S(1)} %collective-permute-done.12), channel_id=1, source_target_pairs={{0,48},{1,17},{2,50},{3,19},{4,52},{5,21},{6,54},{7,23},{8,56},{9,... | collective-permute-start | bytes 1204232 | tf_op jit(solution)/shard_map/ppermute | solution.py:23
  77.9 17.2 %collective-permute-start.26 = (f16[224,896]{1,0:T(8,128)(2,1)S(1)}, f16[224,896]{1,0:T(8,128)(2,1)S(1)}, u32[]{:S(2)}, u32[]{:S(2)}) collective-permute-start(f16[224,896]{1,0:T(8,128)(2,1)S(1)} %collective-permute-done.10), channel_id=1, source_target_pairs={{0,16},{1,49},{2,18},{3,51},{4,20},{5,53},{6,22},{7,55},{8,24},{9,... | collective-permute-start | bytes 1204232 | tf_op jit(solution)/shard_map/ppermute | solution.py:23
  81.7 13.7 %collective-permute-start.27 = (f16[224,896]{1,0:T(8,128)(2,1)S(1)}, f16[224,896]{1,0:T(8,128)(2,1)S(1)}, u32[]{:S(2)}, u32[]{:S(2)}) collective-permute-start(f16[224,896]{1,0:T(8,128)(2,1)S(1)} %collective-permute-done.11), channel_id=1, source_target_pairs={{0,64},{1,193},{2,66},{3,195},{4,68},{5,197},{6,70},{7,199},{8,72}... | collective-permute-start | bytes 1204232 | tf_op jit(solution)/shard_map/ppermute | solution.py:23
  91.8 8.8 %collective-permute-start.24 = (f16[224,896]{1,0:T(8,128)(2,1)S(1)}, f16[224,896]{1,0:T(8,128)(2,1)S(1)}, u32[]{:S(2)}, u32[]{:S(2)}) collective-permute-start(f16[224,896]{1,0:T(8,128)(2,1)S(1)} %collective-permute-done.16), channel_id=1, source_target_pairs={{0,16},{1,49},{2,18},{3,51},{4,20},{5,53},{6,22},{7,55},{8,24},{9,... | collective-permute-start | bytes 1204232 | tf_op jit(solution)/shard_map/ppermute | solution.py:23
  95.2 7.9 %collective-permute-start.25 = (f16[224,896]{1,0:T(8,128)(2,1)S(1)}, f16[224,896]{1,0:T(8,128)(2,1)S(1)}, u32[]{:S(2)}, u32[]{:S(2)}) collective-permute-start(f16[224,896]{1,0:T(8,128)(2,1)S(1)} %collective-permute-done.17), channel_id=1, source_target_pairs={{0,64},{1,193},{2,66},{3,195},{4,68},{5,197},{6,70},{7,199},{8,72}... | collective-permute-start | bytes 1204232 | tf_op jit(solution)/shard_map/ppermute | solution.py:23
where the time goes:
time: 106 us
  starting transfers between devices  45.7 us (43%)
  waiting for transfers between devices  37.9 us (36%)
  Pallas kernels  9.68 us (9%)
  other arithmetic  9.42 us (9%)
  local copies, waits for them, and re-layouts  1.73 us (2%)
  between operations  1.17 us (1%)
    ppermute x30, starting transfers between devices, send(): return lax.ppermute(value, ('rows', 'tp'), pairs)  38.6 us
    ppermute x30, waiting for transfers between devices, send(): return lax.ppermute(value, ('rows', 'tp'), pairs)  36.4 us
    pallas_call x8, Pallas kernels, place(): pl.pallas_call(body, out_shape=tuple((jax.ShapeDtypeStruct(o.shape, o.dty...  9.68 us
    all_to_all x1, starting transfers between devices, per_device(): peaks = lax.all_to_all(peaks, 'rows', 0, 0, tiled=True)  7.04 us
    convert_element_type x32, other arithmetic, decoded(): (code * lax.rsqrt(jnp.maximum(jnp.abs(code), SMALL)) * scale).astype(jnp....  5.8 us
    reduce_max x1, other arithmetic, per_device(): jnp.max(jnp.abs(v), axis=0)  3.21 us
  transfers between devices with their start and end apart: 31, of which 13 were waited for; matrix products, arithmetic and copies ran while one was open for 7% of the time, Pallas kernels for 7%

commit v1 on v0

--- a/solution.py
+++ b/solution.py
@@ -84,18 +84,22 @@
 TOP = 32768.0
 
 SLOTS = (
-    (("gx1", "g", 0, 1), ("uy1", "u", 1, 0), ("ux1", "u", 0, 1), ("gy1", "g", 1, 0)),
-    (("gx2", "g", 0, -1), ("uy2", "u", -1, 0), ("ux2", "u", 0, -1), ("gy2", "g", -1, 0)),
+    (("gx1", "g", 0, 1), ("gy1", "g", 1, 0), ("ux1", "u", 0, 1), ("uy1", "u", 1, 0)),
+    (("gx2", "g", 0, -1), ("uy2", "u", -1, 0)),
+    (("ux2", "u", 0, -1), ("gy2", "g", -1, 0)),
     (("gx3", "gx1", 0, 1), ("uy3", "uy1", 1, 0), ("u11", "uy1", 0, 1), ("g11", "gx1", 1, 0)),
     (("u22", "uy2", 0, -1), ("g22", "gx2", -1, 0), ("ux3", "ux2", 0, -1), ("gy3", "gy2", -1, 0)),
     (("u31", "uy3", 0, 1), ("g31", "gx3", 1, 0), ("u21", "uy2", 0, 1), ("g21", "gx2", 1, 0)),
-    (("u32", "uy3", 0, -1), ("g32", "gx3", -1, 0), ("u23", "u22", 0, -1), ("g23", "g22", -1, 0)),
-    (("u33", "u31", 0, 1), ("g33", "g31", 1, 0), ("u13", "u11", 0, 1), ("g13", "g11", 1, 0)),
-    (("u12", "uy1", 0, -1), ("g12", "gx1", -1, 0)),
+    (
+        ("u13", "u11", 0, 1), ("g13", "g11", 1, 0),
+        ("u32", "uy3", 0, -1), ("g32", "gx3", -1, 0), ("u12", "uy1", 0, -1), ("g12", "gx1", -1, 0),
+    ),
+    (("u23", "u22", 0, -1), ("g23", "g22", -1, 0), ("u33", "u31", 0, 1), ("g33", "g31", 1, 0)),
 )
 ROUTE = tuple(r for slot in SLOTS for r in slot)
 ORIGIN = {"g": (0, 0), "u": (0, 0)}
-BATCHES = [tuple(ORIGIN) + tuple(r[0] for r in SLOTS[0])] + [tuple(r[0] for r in slot) for slot in SLOTS[1:]]
+_ARRIVE = [tuple(r[0] for r in slot) for slot in SLOTS]
+BATCHES = [tuple(ORIGIN) + _ARRIVE[0], _ARRIVE[1] + _ARRIVE[2], *_ARRIVE[3:7], _ARRIVE[7][:2], _ARRIVE[7][2:]]
 for _name, _source, _dy, _dx in ROUTE:
     _y, _x = ORIGIN[_source]
     ORIGIN[_name] = (_y - _dy, _x - _dx)
@@ -104,9 +108,11 @@
 def per_device(train_gate, drift_gate, spread_gate, train_up, drift_up, spread_up, norm_gain):
     rows, width = train_gate.shape
     gate = stepped(train_gate, drift_gate, spread_gate) * norm_gain[:, None]
+    peak_gate = jnp.maximum(jnp.max(jnp.abs(gate), axis=0), SMALL)
+    have = {"g": coded(gate, peak_gate)}
     up = stepped(train_up, drift_up, spread_up) * norm_gain[:, None]
-    peak_gate, peak_up = (jnp.maximum(jnp.max(jnp.abs(v), axis=0), SMALL) for v in (gate, up))
-    have = {"g": coded(gate, peak_gate), "u": coded(up, peak_up)}
+    peak_up = jnp.maximum(jnp.max(jnp.abs(up), axis=0), SMALL)
+    have["u"] = coded(up, peak_up)
     peak = jnp.concatenate([peak_gate, peak_up])
     peaks = jnp.broadcast_to(peak, (SIDE * SIDE, 2 * width))
     peaks = lax.all_to_all(peaks, "rows", 0, 0, tiled=True)

time: 106 us -> 103 us (0.972)
  the two profiles are of different devices: /device:TPU:140 before, /device:TPU:4 now
where the time goes in v1:
time: 103 us
  starting transfers between devices  51.4 us (50%)
  waiting for transfers between devices  29.6 us (29%)
  Pallas kernels  9.68 us (9%)
  other arithmetic  9.42 us (9%)
  local copies, waits for them, and re-layouts  1.73 us (2%)
  between operations  1.16 us (1%)
    ppermute x30, starting transfers between devices, send(): return lax.ppermute(value, ('rows', 'tp'), pairs)  44.3 us
    ppermute x30, waiting for transfers between devices, send(): return lax.ppermute(value, ('rows', 'tp'), pairs)  27.2 us
    pallas_call x8, Pallas kernels, place(): pl.pallas_call(body, out_shape=tuple((jax.ShapeDtypeStruct(o.shape, o.dty...  9.68 us
    all_to_all x1, starting transfers between devices, per_device(): peaks = lax.all_to_all(peaks, 'rows', 0, 0, tiled=True)  7.16 us
    convert_element_type x32, other arithmetic, decoded(): (code * lax.rsqrt(jnp.maximum(jnp.abs(code), SMALL)) * scale).astype(jnp....  5.8 us
    reduce_max x1, other arithmetic, per_device(): peak_up = jnp.maximum(jnp.max(jnp.abs(up), axis=0), SMALL)  3.21 us
    all_to_all x1, waiting for transfers between devices, per_device(): peaks = lax.all_to_all(peaks, 'rows', 0, 0, tiled=True)  2.36 us
  transfers between devices with their start and end apart: 31, of which 13 were waited for; matrix products, arithmetic and copies ran while one was open for 7% of the time, Pallas kernels for 8%

profile of v1, /device:TPU:4, one launch (start us, length us, event | category | flops | bytes accessed | tf_op | source)
XLA Modules:
  0.0 103.0 jit_solution(10677302685355548655)
XLA Ops:
  0.6 3.2 %abs_reduce_fusion = (f32[896]{0:T(1024)S(1)}, f32[224,896]{1,0:T(8,128)S(1)}, f32[896]{0:T(1024)S(1)}, f32[224,896]{1,0:T(8,128)S(1)}) fusion(f32[224]{0:T(256)} %param.13, f32[224,896]{1,0:T(8,128)} %param.10, f32[224,896]{1,0:T(8,128)} %param.11, f32[224,896]{1,0:T(8,128)} %param.12, f32[224,896]{1,0:T(8,128)} %param.7, f32[224,896]{1,0:T(8,128)} %param.8, ...), kind=kLoop, calls=%fused_computation.198 | loop fusion | flops 3610880 | bytes 6430592 | tf_op jit(solution)/shard_map/reduce_max | solution.py:114
  4.0 1.7 %collective-permute-start.3 = (f16[224,896]{1,0:T(8,128)(2,1)S(1)}, f16[224,896]{1,0:T(8,128)(2,1)S(1)}, u32[]{:S(2)}, u32[]{:S(2)}) collective-permute-start(f16[224,896]{1,0:T(8,128)(2,1)S(1)} %fusion.131), channel_id=1, source_target_pairs={{0,64},{1,193},{2,66},{3,195},{4,68},{5,197},{6,70},{7,199},{8,72}... | collective-permute-start | bytes 1204232 | tf_op jit(solution)/shard_map/ppermute | solution.py:23
  7.6 7.2 %all-to-all-start = ((f32[16,1,1792]{2,1,0:T(1,128)}), f32[16,1,1792]{2,1,0:T(1,128)S(1)}, u32[]{:S(2)}, u32[]{:S(2)}) async-start(f32[16,1,1792]{2,1,0:T(1,128)} %broadcast_in_dim.2), calls=%async_computation | async-start | bytes 229376 | tf_op jit(solution)/shard_map/all_to_all | solution.py:118
  14.9 1.5 %collective-permute-start.1 = (f16[224,896]{1,0:T(8,128)(2,1)S(1)}, f16[224,896]{1,0:T(8,128)(2,1)S(1)}, u32[]{:S(2)}, u32[]{:S(2)}) collective-permute-start(f16[224,896]{1,0:T(8,128)(2,1)S(1)} %fusion.129), channel_id=1, source_target_pairs={{0,64},{1,193},{2,66},{3,195},{4,68},{5,197},{6,70},{7,199},{8,72}... | collective-permute-start | bytes 1204232 | tf_op jit(solution)/shard_map/ppermute | solution.py:23
  18.5 2.4 %all-to-all-done = f32[16,1,1792]{2,1,0:T(1,128)S(1)} async-done(((f32[16,1,1792]{2,1,0:T(1,128)}), f32[16,1,1792]{2,1,0:T(1,128)S(1)}, u32[]{:S(2)}, u32[]{:S(2)}) %all-to-all-start) | async-done | bytes 114720 | tf_op jit(solution)/shard_map/all_to_all | solution.py:118
  23.7 1.4 %collective-permute-start.6 = (f16[224,896]{1,0:T(8,128)(2,1)S(1)}, f16[224,896]{1,0:T(8,128)(2,1)S(1)}, u32[]{:S(2)}, u32[]{:S(2)}) collective-permute-start(f16[224,896]{1,0:T(8,128)(2,1)S(1)} %fusion.131), channel_id=1, source_target_pairs={{0,48},{1,17},{2,50},{3,19},{4,52},{5,21},{6,54},{7,23},{8,56},{9,... | collective-permute-start | bytes 1204232 | tf_op jit(solution)/shard_map/ppermute | solution.py:23
  25.3 2.2 %collective-permute-start.7 = (f16[224,896]{1,0:T(8,128)(2,1)S(1)}, f16[224,896]{1,0:T(8,128)(2,1)S(1)}, u32[]{:S(2)}, u32[]{:S(2)}) collective-permute-start(f16[224,896]{1,0:T(8,128)(2,1)S(1)} %fusion.129), channel_id=1, source_target_pairs={{0,192},{1,65},{2,194},{3,67},{4,196},{5,69},{6,198},{7,71},{8,200... | collective-permute-start | bytes 1204232 | tf_op jit(solution)/shard_map/ppermute | solution.py:23
  28.8 1.5 %shard_map.103 = (bf16[3584,896]{1,0:T(8,128)(2,1)}, bf16[3584,896]{1,0:T(8,128)(2,1)}) custom-call(bf16[3584,896]{1,0:T(8,128)(2,1)} %get-tuple-element.22.refs_0_, bf16[3584,896]{1,0:T(8,128)(2,1)} %get-tuple-element.23.refs_1_, bf16[224,896]{1,0:T(8,128)(2,1)S(1)} %fusion.3.refs_2_, ...), custom_call_target="tpu_custom_call", output_to_operand_aliasing={{0}: (0, {}), {1}: (1, {})} | custom-call | tf_op jit(solution)/shard_map/pallas_call | solution.py:49
  30.3 1.2 %collective-permute-start.8 = (f16[224,896]{1,0:T(8,128)(2,1)S(1)}, f16[224,896]{1,0:T(8,128)(2,1)S(1)}, u32[]{:S(2)}, u32[]{:S(2)}) collective-permute-start(f16[224,896]{1,0:T(8,128)(2,1)S(1)} %collective-permute-done), channel_id=1, source_target_pairs={{0,16},{1,49},{2,18},{3,51},{4,20},{5,53},{6,22},{7,55},{8,24},{9,... | collective-permute-start | bytes 1204232 | tf_op jit(solution)/shard_map/ppermute | solution.py:23
  31.5 1.5 %collective-permute-start.9 = (f16[224,896]{1,0:T(8,128)(2,1)S(1)}, f16[224,896]{1,0:T(8,128)(2,1)S(1)}, u32[]{:S(2)}, u32[]{:S(2)}) collective-permute-start(f16[224,896]{1,0:T(8,128)(2,1)S(1)} %collective-permute-done.3), channel_id=1, source_target_pairs={{0,64},{1,193},{2,66},{3,195},{4,68},{5,197},{6,70},{7,199},{8,72}... | collective-permute-start | bytes 1204232 | tf_op jit(solution)/shard_map/ppermute | solution.py:23
  33.8 5.7 %collective-permute-done.7 = f16[224,896]{1,0:T(8,128)(2,1)S(1)} collective-permute-done((f16[224,896]{1,0:T(8,128)(2,1)S(1)}, f16[224,896]{1,0:T(8,128)(2,1)S(1)}, u32[]{:S(2)}, u32[]{:S(2)}) %collective-permute-start.7) | collective-permute-done | bytes 401440 | tf_op jit(solution)/shard_map/ppermute | solution.py:23
  40.9 2.2 %collective-permute-start.11 = (f16[224,896]{1,0:T(8,128)(2,1)S(1)}, f16[224,896]{1,0:T(8,128)(2,1)S(1)}, u32[]{:S(2)}, u32[]{:S(2)}) collective-permute-start(f16[224,896]{1,0:T(8,128)(2,1)S(1)} %collective-permute-done), channel_id=1, source_target_pairs={{0,64},{1,193},{2,66},{3,195},{4,68},{5,197},{6,70},{7,199},{8,72}... | collective-permute-start | bytes 1204232 | tf_op jit(solution)/shard_map/ppermute | solution.py:23
  43.1 1.5 %collective-permute-start.12 = (f16[224,896]{1,0:T(8,128)(2,1)S(1)}, f16[224,896]{1,0:T(8,128)(2,1)S(1)}, u32[]{:S(2)}, u32[]{:S(2)}) collective-permute-start(f16[224,896]{1,0:T(8,128)(2,1)S(1)} %collective-permute-done.5), channel_id=1, source_target_pairs={{0,48},{1,17},{2,50},{3,19},{4,52},{5,21},{6,54},{7,23},{8,56},{9,... | collective-permute-start | bytes 1204232 | tf_op jit(solution)/shard_map/ppermute | solution.py:23
  44.6 1.6 %collective-permute-start.13 = (f16[224,896]{1,0:T(8,128)(2,1)S(1)}, f16[224,896]{1,0:T(8,128)(2,1)S(1)}, u32[]{:S(2)}, u32[]{:S(2)}) collective-permute-start(f16[224,896]{1,0:T(8,128)(2,1)S(1)} %collective-permute-done.4), channel_id=1, source_target_pairs={{0,192},{1,65},{2,194},{3,67},{4,196},{5,69},{6,198},{7,71},{8,200... | collective-permute-start | bytes 1204232 | tf_op jit(solution)/shard_map/ppermute | solution.py:23
  46.4 1.3 %collective-permute-start.14 = (f16[224,896]{1,0:T(8,128)(2,1)S(1)}, f16[224,896]{1,0:T(8,128)(2,1)S(1)}, u32[]{:S(2)}, u32[]{:S(2)}) collective-permute-start(f16[224,896]{1,0:T(8,128)(2,1)S(1)} %collective-permute-done.6), channel_id=1, source_target_pairs={{0,48},{1,17},{2,50},{3,19},{4,52},{5,21},{6,54},{7,23},{8,56},{9,... | collective-permute-start | bytes 1204232 | tf_op jit(solution)/shard_map/ppermute | solution.py:23
  47.8 5.0 %collective-permute-done.10 = f16[224,896]{1,0:T(8,128)(2,1)S(1)} collective-permute-done((f16[224,896]{1,0:T(8,128)(2,1)S(1)}, f16[224,896]{1,0:T(8,128)(2,1)S(1)}, u32[]{:S(2)}, u32[]{:S(2)}) %collective-permute-start.10) | collective-permute-done | bytes 401440 | tf_op jit(solution)/shard_map/ppermute | solution.py:23
  52.8 2.3 %collective-permute-start.15 = (f16[224,896]{1,0:T(8,128)(2,1)S(1)}, f16[224,896]{1,0:T(8,128)(2,1)S(1)}, u32[]{:S(2)}, u32[]{:S(2)}) collective-permute-start(f16[224,896]{1,0:T(8,128)(2,1)S(1)} %collective-permute-done.7), channel_id=1, source_target_pairs={{0,192},{1,65},{2,194},{3,67},{4,196},{5,69},{6,198},{7,71},{8,200... | collective-permute-start | bytes 1204232 | tf_op jit(solution)/shard_map/ppermute | solution.py:23
  56.1 1.2 %shard_map.105 = (bf16[3584,896]{1,0:T(8,128)(2,1)}, bf16[3584,896]{1,0:T(8,128)(2,1)}) custom-call(bf16[3584,896]{1,0:T(8,128)(2,1)} %get-tuple-element.26.refs_0_, bf16[3584,896]{1,0:T(8,128)(2,1)} %get-tuple-element.27.refs_1_, bf16[224,896]{1,0:T(8,128)(2,1)S(1)} %fusion.43.refs_2_, ...), custom_call_target="tpu_custom_call", output_to_operand_aliasing={{0}: (0, {}), {1}: (1, {})} | custom-call | tf_op jit(solution)/shard_map/pallas_call | solution.py:49
  57.6 1.5 %collective-permute-start.24 = (f16[224,896]{1,0:T(8,128)(2,1)S(1)}, f16[224,896]{1,0:T(8,128)(2,1)S(1)}, u32[]{:S(2)}, u32[]{:S(2)}) collective-permute-start(f16[224,896]{1,0:T(8,128)(2,1)S(1)} %collective-permute-done.3), channel_id=1, source_target_pairs={{0,48},{1,17},{2,50},{3,19},{4,52},{5,21},{6,54},{7,23},{8,56},{9,... | collective-permute-start | bytes 1204232 | tf_op jit(solution)/shard_map/ppermute | solution.py:23
  60.2 3.0 %collective-permute-start.25 = (f16[224,896]{1,0:T(8,128)(2,1)S(1)}, f16[224,896]{1,0:T(8,128)(2,1)S(1)}, u32[]{:S(2)}, u32[]{:S(2)}) collective-permute-start(f16[224,896]{1,0:T(8,128)(2,1)S(1)} %collective-permute-done), channel_id=1, source_target_pairs={{0,192},{1,65},{2,194},{3,67},{4,196},{5,69},{6,198},{7,71},{8,200... | collective-permute-start | bytes 1204232 | tf_op jit(solution)/shard_map/ppermute | solution.py:23
  63.4 1.4 %collective-permute-done.15 = f16[224,896]{1,0:T(8,128)(2,1)S(1)} collective-permute-done((f16[224,896]{1,0:T(8,128)(2,1)S(1)}, f16[224,896]{1,0:T(8,128)(2,1)S(1)}, u32[]{:S(2)}, u32[]{:S(2)}) %collective-permute-start.15) | collective-permute-done | bytes 401440 | tf_op jit(solution)/shard_map/ppermute | solution.py:23
  65.0 1.2 %shard_map.106 = (bf16[3584,896]{1,0:T(8,128)(2,1)}, bf16[3584,896]{1,0:T(8,128)(2,1)}) custom-call(bf16[3584,896]{1,0:T(8,128)(2,1)} %get-tuple-element.28.refs_0_, bf16[3584,896]{1,0:T(8,128)(2,1)} %get-tuple-element.29.refs_1_, bf16[224,896]{1,0:T(8,128)(2,1)S(1)} %fusion.59.refs_2_, ...), custom_call_target="tpu_custom_call", output_to_operand_aliasing={{0}: (0, {}), {1}: (1, {})} | custom-call | tf_op jit(solution)/shard_map/pallas_call | solution.py:49
  66.7 1.8 %collective-permute-start.17 = (f16[224,896]{1,0:T(8,128)(2,1)S(1)}, f16[224,896]{1,0:T(8,128)(2,1)S(1)}, u32[]{:S(2)}, u32[]{:S(2)}) collective-permute-start(f16[224,896]{1,0:T(8,128)(2,1)S(1)} %collective-permute-done.8), channel_id=1, source_target_pairs={{0,64},{1,193},{2,66},{3,195},{4,68},{5,197},{6,70},{7,199},{8,72}... | collective-permute-start | bytes 1204232 | tf_op jit(solution)/shard_map/ppermute | solution.py:23
  70.6 2.9 %collective-permute-start.20 = (f16[224,896]{1,0:T(8,128)(2,1)S(1)}, f16[224,896]{1,0:T(8,128)(2,1)S(1)}, u32[]{:S(2)}, u32[]{:S(2)}) collective-permute-start(f16[224,896]{1,0:T(8,128)(2,1)S(1)} %collective-permute-done.10), channel_id=1, source_target_pairs={{0,16},{1,49},{2,18},{3,51},{4,20},{5,53},{6,22},{7,55},{8,24},{9,... | collective-permute-start | bytes 1204232 | tf_op jit(solution)/shard_map/ppermute | solution.py:23
  74.8 3.7 %collective-permute-done.16 = f16[224,896]{1,0:T(8,128)(2,1)S(1)} collective-permute-done((f16[224,896]{1,0:T(8,128)(2,1)S(1)}, f16[224,896]{1,0:T(8,128)(2,1)S(1)}, u32[]{:S(2)}, u32[]{:S(2)}) %collective-permute-start.16) | collective-permute-done | bytes 401440 | tf_op jit(solution)/shard_map/ppermute | solution.py:23
  78.9 2.8 %collective-permute-start.26 = (f16[224,896]{1,0:T(8,128)(2,1)S(1)}, f16[224,896]{1,0:T(8,128)(2,1)S(1)}, u32[]{:S(2)}, u32[]{:S(2)}) collective-permute-start(f16[224,896]{1,0:T(8,128)(2,1)S(1)} %collective-permute-done.12), channel_id=1, source_target_pairs={{0,48},{1,17},{2,50},{3,19},{4,52},{5,21},{6,54},{7,23},{8,56},{9,... | collective-permute-start | bytes 1204232 | tf_op jit(solution)/shard_map/ppermute | solution.py:23
  83.0 2.5 %collective-permute-start.27 = (f16[224,896]{1,0:T(8,128)(2,1)S(1)}, f16[224,896]{1,0:T(8,128)(2,1)S(1)}, u32[]{:S(2)}, u32[]{:S(2)}) collective-permute-start(f16[224,896]{1,0:T(8,128)(2,1)S(1)} %collective-permute-done.13), channel_id=1, source_target_pairs={{0,192},{1,65},{2,194},{3,67},{4,196},{5,69},{6,198},{7,71},{8,200... | collective-permute-start | bytes 1204232 | tf_op jit(solution)/shard_map/ppermute | solution.py:23
  86.1 1.8 %collective-permute-done.22 = f16[224,896]{1,0:T(8,128)(2,1)S(1)} collective-permute-done((f16[224,896]{1,0:T(8,128)(2,1)S(1)}, f16[224,896]{1,0:T(8,128)(2,1)S(1)}, u32[]{:S(2)}, u32[]{:S(2)}) %collective-permute-start.22) | collective-permute-done | bytes 401440 | tf_op jit(solution)/shard_map/ppermute | solution.py:23
  88.1 1.5 %shard_map.108 = (bf16[3584,896]{1,0:T(8,128)(2,1)}, bf16[3584,896]{1,0:T(8,128)(2,1)}) custom-call(bf16[3584,896]{1,0:T(8,128)(2,1)} %get-tuple-element.32.refs_0_, bf16[3584,896]{1,0:T(8,128)(2,1)} %get-tuple-element.33.refs_1_, bf16[224,896]{1,0:T(8,128)(2,1)S(1)} %fusion.91.refs_2_, ...), custom_call_target="tpu_custom_call", output_to_operand_aliasing={{0}: (0, {}), {1}: (1, {})} | custom-call | tf_op jit(solution)/shard_map/pallas_call | solution.py:49
  89.6 3.0 %collective-permute-start.28 = (f16[224,896]{1,0:T(8,128)(2,1)S(1)}, f16[224,896]{1,0:T(8,128)(2,1)S(1)}, u32[]{:S(2)}, u32[]{:S(2)}) collective-permute-start(f16[224,896]{1,0:T(8,128)(2,1)S(1)} %collective-permute-done.16), channel_id=1, source_target_pairs={{0,16},{1,49},{2,18},{3,51},{4,20},{5,53},{6,22},{7,55},{8,24},{9,... | collective-permute-start | bytes 1204232 | tf_op jit(solution)/shard_map/ppermute | solution.py:23
  94.9 3.1 %collective-permute-done.28 = f16[224,896]{1,0:T(8,128)(2,1)S(1)} collective-permute-done((f16[224,896]{1,0:T(8,128)(2,1)S(1)}, f16[224,896]{1,0:T(8,128)(2,1)S(1)}, u32[]{:S(2)}, u32[]{:S(2)}) %collective-permute-start.28) | collective-permute-done | bytes 401440 | tf_op jit(solution)/shard_map/ppermute | solution.py:23
  98.2 3.5 %collective-permute-done.29 = f16[224,896]{1,0:T(8,128)(2,1)S(1)} collective-permute-done((f16[224,896]{1,0:T(8,128)(2,1)S(1)}, f16[224,896]{1,0:T(8,128)(2,1)S(1)}, u32[]{:S(2)}, u32[]{:S(2)}) %collective-permute-start.29) | collective-permute-done | bytes 401440 | tf_op jit(solution)/shard_map/ppermute | solution.py:23
  (84 shorter events, 23.7 us)
Async XLA Ops:
  4.0 18.3 %collective-permute-start.3 = (f16[224,896]{1,0:T(8,128)(2,1)S(1)}, f16[224,896]{1,0:T(8,128)(2,1)S(1)}, u32[]{:S(2)}, u32[]{:S(2)}) collective-permute-start(f16[224,896]{1,0:T(8,128)(2,1)S(1)} %fusion.131), channel_id=1, source_target_pairs={{0,64},{1,193},{2,66},{3,195},{4,68},{5,197},{6,70},{7,199},{8,72}... | collective-permute-start | bytes 1204232 | tf_op jit(solution)/shard_map/ppermute | solution.py:23
  5.7 18.0 %collective-permute-start.2 = (f16[224,896]{1,0:T(8,128)(2,1)S(1)}, f16[224,896]{1,0:T(8,128)(2,1)S(1)}, u32[]{:S(2)}, u32[]{:S(2)}) collective-permute-start(f16[224,896]{1,0:T(8,128)(2,1)S(1)} %fusion.131), channel_id=1, source_target_pairs={{0,16},{1,49},{2,18},{3,51},{4,20},{5,53},{6,22},{7,55},{8,24},{9,... | collective-permute-start | bytes 1204232 | tf_op jit(solution)/shard_map/ppermute | solution.py:23
  7.6 13.2 %all-to-all-start = ((f32[16,1,1792]{2,1,0:T(1,128)}), f32[16,1,1792]{2,1,0:T(1,128)S(1)}, u32[]{:S(2)}, u32[]{:S(2)}) async-start(f32[16,1,1792]{2,1,0:T(1,128)} %broadcast_in_dim.2), calls=%async_computation | async-start | bytes 229376 | tf_op jit(solution)/shard_map/all_to_all | solution.py:118
  14.9 10.4 %collective-permute-start.1 = (f16[224,896]{1,0:T(8,128)(2,1)S(1)}, f16[224,896]{1,0:T(8,128)(2,1)S(1)}, u32[]{:S(2)}, u32[]{:S(2)}) collective-permute-start(f16[224,896]{1,0:T(8,128)(2,1)S(1)} %fusion.129), channel_id=1, source_target_pairs={{0,64},{1,193},{2,66},{3,195},{4,68},{5,197},{6,70},{7,199},{8,72}... | collective-permute-start | bytes 1204232 | tf_op jit(solution)/shard_map/ppermute | solution.py:23
  16.4 12.2 %collective-permute-start = (f16[224,896]{1,0:T(8,128)(2,1)S(1)}, f16[224,896]{1,0:T(8,128)(2,1)S(1)}, u32[]{:S(2)}, u32[]{:S(2)}) collective-permute-start(f16[224,896]{1,0:T(8,128)(2,1)S(1)} %fusion.129), channel_id=1, source_target_pairs={{0,16},{1,49},{2,18},{3,51},{4,20},{5,53},{6,22},{7,55},{8,24},{9,... | collective-permute-start | bytes 1204232 | tf_op jit(solution)/shard_map/ppermute | solution.py:23
  17.6 13.9 %collective-permute-start.4 = (f16[224,896]{1,0:T(8,128)(2,1)S(1)}, f16[224,896]{1,0:T(8,128)(2,1)S(1)}, u32[]{:S(2)}, u32[]{:S(2)}) collective-permute-start(f16[224,896]{1,0:T(8,128)(2,1)S(1)} %fusion.129), channel_id=1, source_target_pairs={{0,48},{1,17},{2,50},{3,19},{4,52},{5,21},{6,54},{7,23},{8,56},{9,... | collective-permute-start | bytes 1204232 | tf_op jit(solution)/shard_map/ppermute | solution.py:23
  22.4 10.8 %collective-permute-start.5 = (f16[224,896]{1,0:T(8,128)(2,1)S(1)}, f16[224,896]{1,0:T(8,128)(2,1)S(1)}, u32[]{:S(2)}, u32[]{:S(2)}) collective-permute-start(f16[224,896]{1,0:T(8,128)(2,1)S(1)} %fusion.131), channel_id=1, source_target_pairs={{0,192},{1,65},{2,194},{3,67},{4,196},{5,69},{6,198},{7,71},{8,200... | collective-permute-start | bytes 1204232 | tf_op jit(solution)/shard_map/ppermute | solution.py:23
  23.7 9.9 %collective-permute-start.6 = (f16[224,896]{1,0:T(8,128)(2,1)S(1)}, f16[224,896]{1,0:T(8,128)(2,1)S(1)}, u32[]{:S(2)}, u32[]{:S(2)}) collective-permute-start(f16[224,896]{1,0:T(8,128)(2,1)S(1)} %fusion.131), channel_id=1, source_target_pairs={{0,48},{1,17},{2,50},{3,19},{4,52},{5,21},{6,54},{7,23},{8,56},{9,... | collective-permute-start | bytes 1204232 | tf_op jit(solution)/shard_map/ppermute | solution.py:23
  25.3 14.1 %collective-permute-start.7 = (f16[224,896]{1,0:T(8,128)(2,1)S(1)}, f16[224,896]{1,0:T(8,128)(2,1)S(1)}, u32[]{:S(2)}, u32[]{:S(2)}) collective-permute-start(f16[224,896]{1,0:T(8,128)(2,1)S(1)} %fusion.129), channel_id=1, source_target_pairs={{0,192},{1,65},{2,194},{3,67},{4,196},{5,69},{6,198},{7,71},{8,200... | collective-permute-start | bytes 1204232 | tf_op jit(solution)/shard_map/ppermute | solution.py:23
  30.3 14.3 %collective-permute-start.8 = (f16[224,896]{1,0:T(8,128)(2,1)S(1)}, f16[224,896]{1,0:T(8,128)(2,1)S(1)}, u32[]{:S(2)}, u32[]{:S(2)}) collective-permute-start(f16[224,896]{1,0:T(8,128)(2,1)S(1)} %collective-permute-done), channel_id=1, source_target_pairs={{0,16},{1,49},{2,18},{3,51},{4,20},{5,53},{6,22},{7,55},{8,24},{9,... | collective-permute-start | bytes 1204232 | tf_op jit(solution)/shard_map/ppermute | solution.py:23
  31.5 14.8 %collective-permute-start.9 = (f16[224,896]{1,0:T(8,128)(2,1)S(1)}, f16[224,896]{1,0:T(8,128)(2,1)S(1)}, u32[]{:S(2)}, u32[]{:S(2)}) collective-permute-start(f16[224,896]{1,0:T(8,128)(2,1)S(1)} %collective-permute-done.3), channel_id=1, source_target_pairs={{0,64},{1,193},{2,66},{3,195},{4,68},{5,197},{6,70},{7,199},{8,72}... | collective-permute-start | bytes 1204232 | tf_op jit(solution)/shard_map/ppermute | solution.py:23
  40.8 11.9 %collective-permute-start.10 = (f16[224,896]{1,0:T(8,128)(2,1)S(1)}, f16[224,896]{1,0:T(8,128)(2,1)S(1)}, u32[]{:S(2)}, u32[]{:S(2)}) collective-permute-start(f16[224,896]{1,0:T(8,128)(2,1)S(1)} %collective-permute-done.3), channel_id=1, source_target_pairs={{0,16},{1,49},{2,18},{3,51},{4,20},{5,53},{6,22},{7,55},{8,24},{9,... | collective-permute-start | bytes 1204232 | tf_op jit(solution)/shard_map/ppermute | solution.py:23
  40.9 14.3 %collective-permute-start.11 = (f16[224,896]{1,0:T(8,128)(2,1)S(1)}, f16[224,896]{1,0:T(8,128)(2,1)S(1)}, u32[]{:S(2)}, u32[]{:S(2)}) collective-permute-start(f16[224,896]{1,0:T(8,128)(2,1)S(1)} %collective-permute-done), channel_id=1, source_target_pairs={{0,64},{1,193},{2,66},{3,195},{4,68},{5,197},{6,70},{7,199},{8,72}... | collective-permute-start | bytes 1204232 | tf_op jit(solution)/shard_map/ppermute | solution.py:23
  43.1 14.2 %collective-permute-start.12 = (f16[224,896]{1,0:T(8,128)(2,1)S(1)}, f16[224,896]{1,0:T(8,128)(2,1)S(1)}, u32[]{:S(2)}, u32[]{:S(2)}) collective-permute-start(f16[224,896]{1,0:T(8,128)(2,1)S(1)} %collective-permute-done.5), channel_id=1, source_target_pairs={{0,48},{1,17},{2,50},{3,19},{4,52},{5,21},{6,54},{7,23},{8,56},{9,... | collective-permute-start | bytes 1204232 | tf_op jit(solution)/shard_map/ppermute | solution.py:23
  44.6 13.0 %collective-permute-start.13 = (f16[224,896]{1,0:T(8,128)(2,1)S(1)}, f16[224,896]{1,0:T(8,128)(2,1)S(1)}, u32[]{:S(2)}, u32[]{:S(2)}) collective-permute-start(f16[224,896]{1,0:T(8,128)(2,1)S(1)} %collective-permute-done.4), channel_id=1, source_target_pairs={{0,192},{1,65},{2,194},{3,67},{4,196},{5,69},{6,198},{7,71},{8,200... | collective-permute-start | bytes 1204232 | tf_op jit(solution)/shard_map/ppermute | solution.py:23
  46.4 13.8 %collective-permute-start.14 = (f16[224,896]{1,0:T(8,128)(2,1)S(1)}, f16[224,896]{1,0:T(8,128)(2,1)S(1)}, u32[]{:S(2)}, u32[]{:S(2)}) collective-permute-start(f16[224,896]{1,0:T(8,128)(2,1)S(1)} %collective-permute-done.6), channel_id=1, source_target_pairs={{0,48},{1,17},{2,50},{3,19},{4,52},{5,21},{6,54},{7,23},{8,56},{9,... | collective-permute-start | bytes 1204232 | tf_op jit(solution)/shard_map/ppermute | solution.py:23
  52.8 12.1 %collective-permute-start.15 = (f16[224,896]{1,0:T(8,128)(2,1)S(1)}, f16[224,896]{1,0:T(8,128)(2,1)S(1)}, u32[]{:S(2)}, u32[]{:S(2)}) collective-permute-start(f16[224,896]{1,0:T(8,128)(2,1)S(1)} %collective-permute-done.7), channel_id=1, source_target_pairs={{0,192},{1,65},{2,194},{3,67},{4,196},{5,69},{6,198},{7,71},{8,200... | collective-permute-start | bytes 1204232 | tf_op jit(solution)/shard_map/ppermute | solution.py:23
  55.2 11.5 %collective-permute-start.18 = (f16[224,896]{1,0:T(8,128)(2,1)S(1)}, f16[224,896]{1,0:T(8,128)(2,1)S(1)}, u32[]{:S(2)}, u32[]{:S(2)}) collective-permute-start(f16[224,896]{1,0:T(8,128)(2,1)S(1)} %collective-permute-done.5), channel_id=1, source_target_pairs={{0,16},{1,49},{2,18},{3,51},{4,20},{5,53},{6,22},{7,55},{8,24},{9,... | collective-permute-start | bytes 1204232 | tf_op jit(solution)/shard_map/ppermute | solution.py:23
  57.3 12.2 %collective-permute-start.19 = (f16[224,896]{1,0:T(8,128)(2,1)S(1)}, f16[224,896]{1,0:T(8,128)(2,1)S(1)}, u32[]{:S(2)}, u32[]{:S(2)}) collective-permute-start(f16[224,896]{1,0:T(8,128)(2,1)S(1)} %collective-permute-done.4), channel_id=1, source_target_pairs={{0,64},{1,193},{2,66},{3,195},{4,68},{5,197},{6,70},{7,199},{8,72}... | collective-permute-start | bytes 1204232 | tf_op jit(solution)/shard_map/ppermute | solution.py:23
  57.6 13.0 %collective-permute-start.24 = (f16[224,896]{1,0:T(8,128)(2,1)S(1)}, f16[224,896]{1,0:T(8,128)(2,1)S(1)}, u32[]{:S(2)}, u32[]{:S(2)}) collective-permute-start(f16[224,896]{1,0:T(8,128)(2,1)S(1)} %collective-permute-done.3), channel_id=1, source_target_pairs={{0,48},{1,17},{2,50},{3,19},{4,52},{5,21},{6,54},{7,23},{8,56},{9,... | collective-permute-start | bytes 1204232 | tf_op jit(solution)/shard_map/ppermute | solution.py:23
  60.2 13.6 %collective-permute-start.25 = (f16[224,896]{1,0:T(8,128)(2,1)S(1)}, f16[224,896]{1,0:T(8,128)(2,1)S(1)}, u32[]{:S(2)}, u32[]{:S(2)}) collective-permute-start(f16[224,896]{1,0:T(8,128)(2,1)S(1)} %collective-permute-done), channel_id=1, source_target_pairs={{0,192},{1,65},{2,194},{3,67},{4,196},{5,69},{6,198},{7,71},{8,200... | collective-permute-start | bytes 1204232 | tf_op jit(solution)/shard_map/ppermute | solution.py:23
  66.3 12.2 %collective-permute-start.16 = (f16[224,896]{1,0:T(8,128)(2,1)S(1)}, f16[224,896]{1,0:T(8,128)(2,1)S(1)}, u32[]{:S(2)}, u32[]{:S(2)}) collective-permute-start(f16[224,896]{1,0:T(8,128)(2,1)S(1)} %collective-permute-done.9), channel_id=1, source_target_pairs={{0,16},{1,49},{2,18},{3,51},{4,20},{5,53},{6,22},{7,55},{8,24},{9,... | collective-permute-start | bytes 1204232 | tf_op jit(solution)/shard_map/ppermute | solution.py:23
  66.7 12.1 %collective-permute-start.17 = (f16[224,896]{1,0:T(8,128)(2,1)S(1)}, f16[224,896]{1,0:T(8,128)(2,1)S(1)}, u32[]{:S(2)}, u32[]{:S(2)}) collective-permute-start(f16[224,896]{1,0:T(8,128)(2,1)S(1)} %collective-permute-done.8), channel_id=1, source_target_pairs={{0,64},{1,193},{2,66},{3,195},{4,68},{5,197},{6,70},{7,199},{8,72}... | collective-permute-start | bytes 1204232 | tf_op jit(solution)/shard_map/ppermute | solution.py:23
  69.5 13.5 %collective-permute-start.23 = (f16[224,896]{1,0:T(8,128)(2,1)S(1)}, f16[224,896]{1,0:T(8,128)(2,1)S(1)}, u32[]{:S(2)}, u32[]{:S(2)}) collective-permute-start(f16[224,896]{1,0:T(8,128)(2,1)S(1)} %collective-permute-done.8), channel_id=1, source_target_pairs={{0,192},{1,65},{2,194},{3,67},{4,196},{5,69},{6,198},{7,71},{8,200... | collective-permute-start | bytes 1204232 | tf_op jit(solution)/shard_map/ppermute | solution.py:23
  70.6 15.0 %collective-permute-start.20 = (f16[224,896]{1,0:T(8,128)(2,1)S(1)}, f16[224,896]{1,0:T(8,128)(2,1)S(1)}, u32[]{:S(2)}, u32[]{:S(2)}) collective-permute-start(f16[224,896]{1,0:T(8,128)(2,1)S(1)} %collective-permute-done.10), channel_id=1, source_target_pairs={{0,16},{1,49},{2,18},{3,51},{4,20},{5,53},{6,22},{7,55},{8,24},{9,... | collective-permute-start | bytes 1204232 | tf_op jit(solution)/shard_map/ppermute | solution.py:23
  73.8 12.1 %collective-permute-start.21 = (f16[224,896]{1,0:T(8,128)(2,1)S(1)}, f16[224,896]{1,0:T(8,128)(2,1)S(1)}, u32[]{:S(2)}, u32[]{:S(2)}) collective-permute-start(f16[224,896]{1,0:T(8,128)(2,1)S(1)} %collective-permute-done.11), channel_id=1, source_target_pairs={{0,64},{1,193},{2,66},{3,195},{4,68},{5,197},{6,70},{7,199},{8,72}... | collective-permute-start | bytes 1204232 | tf_op jit(solution)/shard_map/ppermute | solution.py:23
  78.5 9.4 %collective-permute-start.22 = (f16[224,896]{1,0:T(8,128)(2,1)S(1)}, f16[224,896]{1,0:T(8,128)(2,1)S(1)}, u32[]{:S(2)}, u32[]{:S(2)}) collective-permute-start(f16[224,896]{1,0:T(8,128)(2,1)S(1)} %collective-permute-done.9), channel_id=1, source_target_pairs={{0,48},{1,17},{2,50},{3,19},{4,52},{5,21},{6,54},{7,23},{8,56},{9,... | collective-permute-start | bytes 1204232 | tf_op jit(solution)/shard_map/ppermute | solution.py:23
  78.9 14.7 %collective-permute-start.26 = (f16[224,896]{1,0:T(8,128)(2,1)S(1)}, f16[224,896]{1,0:T(8,128)(2,1)S(1)}, u32[]{:S(2)}, u32[]{:S(2)}) collective-permute-start(f16[224,896]{1,0:T(8,128)(2,1)S(1)} %collective-permute-done.12), channel_id=1, source_target_pairs={{0,48},{1,17},{2,50},{3,19},{4,52},{5,21},{6,54},{7,23},{8,56},{9,... | collective-permute-start | bytes 1204232 | tf_op jit(solution)/shard_map/ppermute | solution.py:23
  83.0 10.7 %collective-permute-start.27 = (f16[224,896]{1,0:T(8,128)(2,1)S(1)}, f16[224,896]{1,0:T(8,128)(2,1)S(1)}, u32[]{:S(2)}, u32[]{:S(2)}) collective-permute-start(f16[224,896]{1,0:T(8,128)(2,1)S(1)} %collective-permute-done.13), channel_id=1, source_target_pairs={{0,192},{1,65},{2,194},{3,67},{4,196},{5,69},{6,198},{7,71},{8,200... | collective-permute-start | bytes 1204232 | tf_op jit(solution)/shard_map/ppermute | solution.py:23
  89.6 8.4 %collective-permute-start.28 = (f16[224,896]{1,0:T(8,128)(2,1)S(1)}, f16[224,896]{1,0:T(8,128)(2,1)S(1)}, u32[]{:S(2)}, u32[]{:S(2)}) collective-permute-start(f16[224,896]{1,0:T(8,128)(2,1)S(1)} %collective-permute-done.16), channel_id=1, source_target_pairs={{0,16},{1,49},{2,18},{3,51},{4,20},{5,53},{6,22},{7,55},{8,24},{9,... | collective-permute-start | bytes 1204232 | tf_op jit(solution)/shard_map/ppermute | solution.py:23
  92.6 9.1 %collective-permute-start.29 = (f16[224,896]{1,0:T(8,128)(2,1)S(1)}, f16[224,896]{1,0:T(8,128)(2,1)S(1)}, u32[]{:S(2)}, u32[]{:S(2)}) collective-permute-start(f16[224,896]{1,0:T(8,128)(2,1)S(1)} %collective-permute-done.17), channel_id=1, source_target_pairs={{0,64},{1,193},{2,66},{3,195},{4,68},{5,197},{6,70},{7,199},{8,72}... | collective-permute-start | bytes 1204232 | tf_op jit(solution)/shard_map/ppermute | solution.py:23
